TPU v7x, 32 devices: a whole 2x2x4 slice. The times are simulated.
32 devices in a mesh: gx: 16 (over z, x, core), gy: 2 (over y).
Axes of the slice: x: 2, y: 2, z: 4, core: 2. Of those that a mesh axis runs over, the one named last changes fastest.
Arguments:
- positions: float32 [3, 12, 32, 32, 256], P(None, None, 'gx', 'gy'), may hold values from 0 to 1
- velocities: float32 [3, 12, 32, 32, 256], P(None, None, 'gx', 'gy'), may hold values from -6 to 6
- thermal: float32 [3, 12, 32, 32, 256], P(None, None, 'gx', 'gy'), may hold values from -6 to 6
- offsets: int32 [12, 32, 32, 256], P(None, 'gx', 'gy'), may hold values from 0 to 7
- occupancy: int32 [12, 32, 32, 256], P(None, 'gx', 'gy'), may hold values from 0 to 1, as said below
- shift_codes: int32 [3], replicated, may hold values from 0 to 7
Outputs:
- new_velocities: float32 [3, 12, 32, 32, 256], P(None, None, 'gx', 'gy')
Inputs may be any that keep to these rules, and one draw needn't show every extreme that they name: `occupancy`: the particles of a storage cell occupy its first slots; every storage cell holds 8 to 12 particles.
All inputs are finite; a program needn't handle non-finite values.
Results may differ from a plain program's by a relative error of at most 0.0001.
Values sent between devices are 32-bit elements; how exact they have to be, the bound alone decides.
A program may use at most 64 MiB of HBM per device.

v0:
```python
import functools

import jax
import jax.numpy as jnp
from jax import lax
from jax.experimental import pallas as pl
from jax.experimental.pallas import tpu as pltpu
from jax.sharding import PartitionSpec as P

STEPS = 3
RIDGE = 0.5
F32 = jnp.float32
NS = 10
ND = 6
DIRS = ((-1, 0), (1, 0), (0, -1), (0, 1), (-1, -1), (-1, 1), (1, -1), (1, 1))


def pad8(v):
    return (v + 7) // 8 * 8


def cross(a, b):
    return [
        a[1] * b[2] - a[2] * b[1],
        a[2] * b[0] - a[0] * b[2],
        a[0] * b[1] - a[1] * b[0],
    ]


def translate_static(m, axis):
    n, x, y, z, xx, yy, zz, xy, xz, yz = m
    if axis == 0:
        return [n, x + n, y, z, xx + (x + x) + n, yy, zz, xy + y, xz + z, yz]
    if axis == 1:
        return [n, x, y + n, z, xx, yy + (y + y) + n, zz, xy + x, xz, yz + z]
    return [n, x, y, z + n, xx, yy, zz + (z + z) + n, xy, xz + x, yz + y]


def translate_dynamic(m, axis):
    wx, wy, wz, lx, ly, lz = m
    if axis == 0:
        return [wx, wy, wz, lx, ly - wz, lz + wy]
    if axis == 1:
        return [wx, wy, wz, lx + wz, ly, lz - wx]
    return [wx, wy, wz, lx - wy, ly + wx, lz]


def kernel(
    shift_ref, pos_h, vel_h, th_h, off_h, occ_h, res,
    pos, vel, th, off, occ, grp, upd, est, edy,
    sx_s, sy_s, rx_s, ry_s, rc_s, sx_d, sy_d, rx_d, ry_d, rc_d,
    in_sem, send_sem, recv_sem,
):
    slots, rows, cols, depth = off.shape
    gx, gy = lax.axis_index("gx"), lax.axis_index("gy")
    nx, ny = lax.axis_size("gx"), lax.axis_size("gy")

    def device(dx, dy):
        return (lax.rem(gx + dx + nx, nx), lax.rem(gy + dy + ny, ny))

    loads = [
        pltpu.make_async_copy(src, dst, in_sem.at[k])
        for k, (src, dst) in enumerate(
            ((off_h, off), (occ_h, occ), (pos_h, pos), (th_h, th), (vel_h, vel))
        )
    ]
    for copy in loads:
        copy.start()
    barrier = pltpu.get_barrier_semaphore()
    for dx, dy in DIRS:
        pl.semaphore_signal(
            barrier, inc=1, device_id=device(dx, dy), device_id_type=pl.DeviceIdType.MESH
        )

    yb, zb = cols // 8, depth // 128
    blocks = rows * yb * zb
    code_ids = lax.broadcasted_iota(jnp.int32, (8, 8, 128), 0)

    def place(index):
        r = index // (yb * zb)
        rest = index % (yb * zb)
        y = pl.multiple_of((rest // zb) * 8, 8)
        z = pl.multiple_of((rest % zb) * 128, 128)
        return r, pl.ds(y, 8), pl.ds(z, 128)

    def accumulate(where_at, base, make_terms):
        r, ys, zs = where_at
        total = None
        for m in range(slots):
            mask = code_ids == off[m, r, ys, zs][None]
            terms = make_terms(m)
            picked = [jnp.where(mask, t if isinstance(t, float) else t[None], 0.0) for t in terms]
            total = picked if total is None else [a + b for a, b in zip(total, picked)]
        for k, value in enumerate(total):
            grp[base + k, :, r, ys, zs] = value

    def point(m, at):
        return [pos[(k, m) + at] for k in range(3)]

    for copy in loads[:3]:
        copy.wait()

    def static_block(index, carry):
        at = place(index)
        r, ys, zs = at
        for m in range(slots):
            off[m, r, ys, zs] = jnp.where(occ[m, r, ys, zs] == 1, off[m, r, ys, zs], 8)
        accumulate(at, 0, lambda m: [1.0] + point(m, at))

        def squares(m):
            return [v * v for v in point(m, at)]

        def products(m):
            x, y, z = point(m, at)
            return [x * y, x * z, y * z]

        accumulate(at, 4, squares)
        accumulate(at, 7, products)
        return carry

    def flow_block(step, index, carry):
        at = place(index)

        def flow(m):
            now = [th[(k, (m + step) % slots) + at] for k in range(3)]
            if step == 0:
                before = [vel[(k, m) + at] for k in range(3)]
            else:
                before = [th[(k, (m + step - 1) % slots) + at] for k in range(3)]
            return [a - b for a, b in zip(before, now)]

        accumulate(at, NS + ND * step, flow)
        accumulate(at, NS + ND * step + 3, lambda m: cross(point(m, at), flow(m)))
        return carry

    sub = lax.broadcasted_iota(jnp.int32, (cols, depth), 0)

    def build(load, translate, count, ext, sx, sy):
        vp = pad8(count)

        def merged(e, by):
            halves = []
            for bz in range(2):
                parts = []
                if e > 0:
                    parts.append(load(2 * by + bz, e - 1))
                if e < rows:
                    parts.append(translate(load(4 + 2 * by + bz, e), 0))
                halves.append(parts[0] if len(parts) == 1 else [a + b for a, b in zip(*parts)])
            high = [pltpu.roll(v, depth - 1, 1) for v in translate(halves[1], 2)]
            return [a + b for a, b in zip(halves[0], high)]

        for e in range(rows + 1):
            low = merged(e, 0)
            high = translate(merged(e, 1), 1)
            for v in range(count):
                moved = pltpu.roll(high[v], cols - 1, 0)
                main = low[v] + jnp.where(sub == cols - 1, 0.0, moved)
                rim = high[v][0:1]
                ext[v, e, 0:cols] = main
                ext[v, e, cols : cols + 1] = rim
                for side, row in ((0, 0), (1, rows)):
                    if e == row:
                        sx[side, v * cols : (v + 1) * cols] = main
                        sx[side, count * cols + v : count * cols + v + 1] = rim
                sy[0, e * vp + v : e * vp + v + 1] = rim
                sy[1, e * vp + v : e * vp + v + 1] = main[cols - 1 : cols]

    def copies(count, sx, sy, rx, ry, rc, kind, step):
        vp = pad8(count)
        out = []
        for k, (dx, dy) in enumerate(DIRS):
            if dy == 0:
                src, dst = sx.at[k], rx.at[k]
            elif dx == 0:
                src, dst = sy.at[k - 2], ry.at[k - 2]
            else:
                src = sy.at[0 if dy < 0 else 1, pl.ds((0 if dx < 0 else rows) * vp, vp)]
                dst = rc.at[k - 4]
            out.append(
                pltpu.make_async_remote_copy(
                    src_ref=src, dst_ref=dst,
                    send_sem=send_sem.at[kind, step, k],
                    recv_sem=recv_sem.at[kind, step, k],
                    device_id=device(dx, dy),
                    device_id_type=pl.DeviceIdType.MESH,
                )
            )
        return out

    def absorb(count, ext, rx, ry, rc, sent):
        vp = pad8(count)
        for copy in sent:
            copy.wait_recv()
        for v in range(count):
            for side, e in ((0, rows), (1, 0)):
                ext[v, e, 0:cols] += rx[side, v * cols : (v + 1) * cols]
                ext[v, e, cols : cols + 1] += rx[side, count * cols + v : count * cols + v + 1]
            for e in range(rows + 1):
                for side, row in ((0, cols - 1), (1, cols)):
                    extra = ry[side, e * vp + v : e * vp + v + 1]
                    if e == rows:
                        extra = extra + rc[side, v : v + 1]
                    if e == 0:
                        extra = extra + rc[2 + side, v : v + 1]
                    ext[v, e, row : row + 1] += extra

    def static_solve(ext):
        for e in range(rows + 1):
            n, sx, sy, sz, xx, yy, zz, xy, xz, yz = [ext[v, e] for v in range(NS)]
            inv = 1.0 / jnp.maximum(n, 1.0)
            cx, cy, cz = sx * inv, sy * inv, sz * inv
            mxx, myy, mzz = xx - sx * cx, yy - sy * cy, zz - sz * cz
            kxy, kxz, kyz = sx * cy - xy, sx * cz - xz, sy * cz - yz
            kxx = myy + mzz + RIDGE
            kyy = mxx + mzz + RIDGE
            kzz = mxx + myy + RIDGE
            axx = kyy * kzz - kyz * kyz
            ayy = kxx * kzz - kxz * kxz
            azz = kxx * kyy - kxy * kxy
            axy = kxz * kyz - kxy * kzz
            axz = kxy * kyz - kxz * kyy
            ayz = kxy * kxz - kxx * kyz
            scale = 1.0 / (kxx * axx + kxy * axy + kxz * axz)
            done = [inv, cx, cy, cz] + [a * scale for a in (axx, ayy, azz, axy, axz, ayz)]
            for v in range(NS):
                ext[v, e] = done[v]

    def tables(ext, dyn):
        out = []
        for e in range(rows + 1):
            inv, cx, cy, cz, ixx, iyy, izz, ixy, ixz, iyz = [ext[v, e] for v in range(NS)]
            flow = [dyn[v, e] for v in range(3)]
            centre = [cx, cy, cz]
            tq = [dyn[3 + k, e] - t for k, t in enumerate(cross(centre, flow))]
            spin = [
                ixx * tq[0] + ixy * tq[1] + ixz * tq[2],
                ixy * tq[0] + iyy * tq[1] + iyz * tq[2],
                ixz * tq[0] + iyz * tq[1] + izz * tq[2],
            ]
            base = [f * inv - t for f, t in zip(flow, cross(spin, centre))]
            by_bits = {}
            values = base + spin
            straight = [v[0:cols] for v in values]
            moved = [
                jnp.where(
                    sub == 0,
                    jnp.broadcast_to(v[cols : cols + 1], (cols, depth)),
                    pltpu.roll(v[0:cols], 1, 0),
                )
                for v in values
            ]
            for by, plain in ((0, straight), (1, moved)):
                by_bits[by, 0] = plain
                by_bits[by, 1] = [pltpu.roll(v, 1, 1) for v in plain]
            out.append(by_bits)
        return out

    def solve(step):
        made = tables(est.at[step], edy)
        shift = shift_ref[step]
        for code in range(8):
            bits = (code // 4, code // 2 % 2, code % 2)
            for r in range(rows):
                a0, a1, a2, s0, s1, s2 = made[r - bits[0] + 1][bits[1], bits[2]]
                if bits[2]:
                    a0, a1 = a0 + s1, a1 - s0
                if bits[1]:
                    a0, a2 = a0 - s2, a2 + s0
                if bits[0]:
                    a1, a2 = a1 + s2, a2 - s1
                if step == STEPS - 1:
                    done = [a0, a1, a2, s0, s1, s2]
                else:
                    own = jnp.bitwise_xor(shift, code)
                    n, x, y, z, xx, yy, zz, xy, xz, yz = [grp[v, own, r] for v in range(NS)]
                    turn = cross([s0, s1, s2], [x, y, z])
                    arm = cross([x, y, z], [a0, a1, a2])
                    done = [
                        n * a0 + turn[0],
                        n * a1 + turn[1],
                        n * a2 + turn[2],
                        arm[0] + (yy + zz) * s0 - xy * s1 - xz * s2,
                        arm[1] + (xx + zz) * s1 - xy * s0 - yz * s2,
                        arm[2] + (xx + yy) * s2 - xz * s0 - yz * s1,
                    ]
                for v in range(ND):
                    upd[v, code, r] = done[v]

    def load_static(step):
        shift = shift_ref[step]

        def load(code, r):
            own = jnp.bitwise_xor(shift, code)
            return [grp[v, own, r] for v in range(NS)]

        return load

    def load_dynamic(step):
        shift = shift_ref[step]

        def load(code, r):
            own = jnp.bitwise_xor(shift, code)
            values = [grp[NS + ND * step + v, own, r] for v in range(ND)]
            if step:
                last = jnp.bitwise_xor(own, shift_ref[step - 1])
                values = [a + upd[v, last, r] for v, a in enumerate(values)]
            return values

        return load

    static_sent = [
        copies(NS, sx_s.at[s], sy_s.at[s], rx_s.at[s], ry_s.at[s], rc_s.at[s], 0, s)
        for s in range(STEPS)
    ]
    dynamic_sent = [
        copies(ND, sx_d.at[s], sy_d.at[s], rx_d.at[s], ry_d.at[s], rc_d.at[s], 1, s)
        for s in range(STEPS)
    ]

    def send_static(s):
        build(load_static(s), translate_static, NS, est.at[s], sx_s.at[s], sy_s.at[s])
        for copy in static_sent[s]:
            copy.start()

    def send_dynamic(s):
        build(load_dynamic(s), translate_dynamic, ND, edy, sx_d.at[s], sy_d.at[s])
        for copy in dynamic_sent[s]:
            copy.start()

    def finish_static(s):
        absorb(NS, est.at[s], rx_s.at[s], ry_s.at[s], rc_s.at[s], static_sent[s])
        static_solve(est.at[s])

    lax.fori_loop(0, blocks, static_block, 0)
    pl.semaphore_wait(barrier, len(DIRS))
    send_static(0)
    for copy in loads[3:]:
        copy.wait()
    lax.fori_loop(0, blocks, functools.partial(flow_block, 0), 0)
    send_dynamic(0)
    lax.fori_loop(0, blocks, functools.partial(flow_block, 1), 0)
    lax.fori_loop(0, blocks, functools.partial(flow_block, 2), 0)
    send_static(1)
    finish_static(0)
    for s in range(STEPS):
        absorb(ND, edy, rx_d.at[s], ry_d.at[s], rc_d.at[s], dynamic_sent[s])
        solve(s)
        if s + 1 < STEPS:
            send_dynamic(s + 1)
            if s == 0:
                send_static(2)
            finish_static(s + 1)

    shift = shift_ref[STEPS - 1]
    last_step = STEPS - 1

    def final_block(index, carry):
        at = place(index)
        r, ys, zs = at
        for first in range(0, slots, 6):
            batch = range(first, min(first + 6, slots))
            codes = {m: off[m, r, ys, zs] for m in batch}
            picked = {m: [] for m in batch}
            for v in range(ND):
                leaf = [upd[v, jnp.bitwise_xor(shift, o), r, ys, zs] for o in range(8)]
                for m in batch:
                    one = jnp.bitwise_and(codes[m], 1) == 1
                    two = jnp.bitwise_and(codes[m], 2) == 2
                    four = jnp.bitwise_and(codes[m], 4) == 4
                    level = [jnp.where(one, leaf[k + 1], leaf[k]) for k in range(0, 8, 2)]
                    level = [jnp.where(two, level[k + 1], level[k]) for k in range(0, 4, 2)]
                    picked[m].append(jnp.where(four, level[1], level[0]))
            for m in batch:
                turn = cross(picked[m][3:], point(m, at))
                full = codes[m] < 8
                for k in range(3):
                    hot = th[(k, (m + last_step) % slots) + at]
                    res[k, m, r, ys, zs] = jnp.where(full, hot + picked[m][k] + turn[k], 0.0)
        return carry

    lax.fori_loop(0, blocks, final_block, 0)
    for group in static_sent + dynamic_sent:
        for copy in group:
            copy.wait_send()


def local(positions, velocities, thermal, offsets, occupancy, shift_codes):
    slots, rows, cols, depth = offsets.shape
    full = (3, slots, rows, cols, depth)
    plane = (slots, rows, cols, depth)

    def faces(count):
        vp = pad8(count)
        wide = pltpu.VMEM((STEPS, 2, count * cols + vp, depth), F32)
        thin = pltpu.VMEM((STEPS, 2, (rows + 1) * vp, depth), F32)
        return [wide, thin, wide, thin, pltpu.VMEM((STEPS, 4, vp, depth), F32)]

    hbm = pl.BlockSpec(memory_space=pltpu.HBM)
    return pl.pallas_call(
        kernel,
        out_shape=jax.ShapeDtypeStruct(full, F32),
        in_specs=[pl.BlockSpec(memory_space=pltpu.SMEM)] + [hbm] * 5,
        out_specs=pl.BlockSpec(memory_space=pltpu.VMEM),
        scratch_shapes=[
            pltpu.VMEM(full, F32),
            pltpu.VMEM(full, F32),
            pltpu.VMEM(full, F32),
            pltpu.VMEM(plane, jnp.int32),
            pltpu.VMEM(plane, jnp.int32),
            pltpu.VMEM((NS + ND * STEPS, 8, rows, cols, depth), F32),
            pltpu.VMEM((ND, 8, rows, cols, depth), F32),
            pltpu.VMEM((STEPS, NS, rows + 1, cols + 8, depth), F32),
            pltpu.VMEM((ND, rows + 1, cols + 8, depth), F32),
            *faces(NS),
            *faces(ND),
            pltpu.SemaphoreType.DMA((5,)),
            pltpu.SemaphoreType.DMA((2, STEPS, len(DIRS))),
            pltpu.SemaphoreType.DMA((2, STEPS, len(DIRS))),
        ],
        compiler_params=pltpu.CompilerParams(
            collective_id=0, has_side_effects=True, vmem_limit_bytes=67043328
        ),
    )(shift_codes, positions, velocities, thermal, offsets, occupancy)


def solution(mesh):
    in_specs = (
        P(None, None, "gx", "gy", None),
        P(None, None, "gx", "gy", None),
        P(None, None, "gx", "gy", None),
        P(None, "gx", "gy", None),
        P(None, "gx", "gy", None),
        P(),
    )
    out_specs = P(None, None, "gx", "gy", None)
    return jax.shard_map(local, mesh=mesh, in_specs=in_specs, out_specs=out_specs, check_vma=False)
```

profile of v0, /device:TPU:1, one launch (start us, length us, event | category | flops | bytes accessed | tf_op | source)
XLA Modules:
  0.0 37.8 jit_solution(14580334664379498867)
XLA Ops:
  0.0 35.3 %shard_map.64 = f32[3,12,2,16,256]{4,3,2,1,0:T(8,128)} custom-call(s32[3]{0:T(128)} %shift_ref.1, f32[3,12,2,16,256]{4,3,2,1,0:T(8,128)} %pos_h.1, f32[3,12,2,16,256]{4,3,2,1,0:T(8,128)} %vel_h.1, f32[3,12,2,16,256]{4,3,2,1,0:T(8,128)} %th_h.1, s32[12,2,16,256]{3,2,1,0:T(8,128)} %off_h.1, s32[12,2,16,256]{3,2,1,0:T(8,128)} %occ_h.1), custom_call_target="tpu_custom_call" | custom-call | tf_op jit(solution)/shard_map/pallas_call | solution.py:400
  35.3 2.4 %copy.8 = f32[3,12,2,16,256]{4,3,2,1,0:T(8,128)} copy(f32[3,12,2,16,256]{4,3,2,1,0:T(8,128)} %shard_map.64) | data formatting | bytes 2359296
where the time goes:
time: 37.9 us; the launch traced here: 37.8 us
  Pallas kernels  35.3 us (93%)
  local copies, waits for them, and re-layouts  2.42 us (6%)
    pallas_call x1, Pallas kernels, local(): pl.pallas_call(kernel, out_shape=jax.ShapeDtypeStruct(full, F32), in_spec...  35.3 us
    unnamed x1, local copies, waits for them, and re-layouts  2.42 us

commit v1 on v0

--- a/solution.py
+++ b/solution.py
@@ -46,8 +46,8 @@
 
 
 def kernel(
-    shift_ref, pos_h, vel_h, th_h, off_h, occ_h, res,
-    pos, vel, th, off, occ, grp, upd, est, edy,
+    shift_h, pos_h, vel_h, th_h, off_h, occ_h, res,
+    shift_ref, pos, vel, th, off, occ, grp, upd, est, edy,
     sx_s, sy_s, rx_s, ry_s, rc_s, sx_d, sy_d, rx_d, ry_d, rc_d,
     in_sem, send_sem, recv_sem,
 ):
@@ -61,7 +61,7 @@
     loads = [
         pltpu.make_async_copy(src, dst, in_sem.at[k])
         for k, (src, dst) in enumerate(
-            ((off_h, off), (occ_h, occ), (pos_h, pos), (th_h, th), (vel_h, vel))
+            ((off_h, off), (occ_h, occ), (pos_h, pos), (th_h, th), (vel_h, vel), (shift_h, shift_ref))
         )
     ]
     for copy in loads:
@@ -334,8 +334,9 @@
 
     lax.fori_loop(0, blocks, static_block, 0)
     pl.semaphore_wait(barrier, len(DIRS))
+    loads[5].wait()
     send_static(0)
-    for copy in loads[3:]:
+    for copy in loads[3:5]:
         copy.wait()
     lax.fori_loop(0, blocks, functools.partial(flow_block, 0), 0)
     send_dynamic(0)
@@ -386,6 +387,7 @@
 
 
 def local(positions, velocities, thermal, offsets, occupancy, shift_codes):
+    args = (shift_codes, positions, velocities, thermal, offsets, occupancy)
     slots, rows, cols, depth = offsets.shape
     full = (3, slots, rows, cols, depth)
     plane = (slots, rows, cols, depth)
@@ -399,10 +401,11 @@
     hbm = pl.BlockSpec(memory_space=pltpu.HBM)
     return pl.pallas_call(
         kernel,
-        out_shape=jax.ShapeDtypeStruct(full, F32),
-        in_specs=[pl.BlockSpec(memory_space=pltpu.SMEM)] + [hbm] * 5,
+        out_shape=pltpu.VMEM(full, F32),
+        in_specs=[hbm] * 6,
         out_specs=pl.BlockSpec(memory_space=pltpu.VMEM),
         scratch_shapes=[
+            pltpu.SMEM((STEPS,), jnp.int32),
             pltpu.VMEM(full, F32),
             pltpu.VMEM(full, F32),
             pltpu.VMEM(full, F32),
@@ -414,14 +417,14 @@
             pltpu.VMEM((ND, rows + 1, cols + 8, depth), F32),
             *faces(NS),
             *faces(ND),
-            pltpu.SemaphoreType.DMA((5,)),
+            pltpu.SemaphoreType.DMA((6,)),
             pltpu.SemaphoreType.DMA((2, STEPS, len(DIRS))),
             pltpu.SemaphoreType.DMA((2, STEPS, len(DIRS))),
         ],
         compiler_params=pltpu.CompilerParams(
-            collective_id=0, has_side_effects=True, vmem_limit_bytes=67043328
+            collective_id=0, has_side_effects=True, vmem_limit_bytes=40000000
         ),
-    )(shift_codes, positions, velocities, thermal, offsets, occupancy)
+    )(*[pltpu.with_memory_space_constraint(v, pltpu.HBM) for v in args])
 
 
 def solution(mesh):

time: 37.9 us -> 34.8 us (0.918)
  Pallas kernels: 35.3 us -> 33.6 us
  local copies, waits for them, and re-layouts: 2.42 us -> 1.02 us
    pallas_call x1, Pallas kernels: 35.3 us -> 33.6 us  [local(): pl.pallas_call(kernel, out_shape=pltpu.VMEM(full, F32), in_specs=[hbm] *...]
    unnamed x1, local copies, waits for them, and re-layouts: 2.42 us -> 1.02 us
where the time goes in v1:
time: 34.8 us; the launch traced here: 34.7 us
  Pallas kernels  33.6 us (97%)
  local copies, waits for them, and re-layouts  1.02 us (3%)
    pallas_call x1, Pallas kernels, local(): pl.pallas_call(kernel, out_shape=pltpu.VMEM(full, F32), in_specs=[hbm] *...  33.6 us
    unnamed x1, local copies, waits for them, and re-layouts  1.02 us

profile of v1, /device:TPU:1, one launch (start us, length us, event | category | flops | bytes accessed | tf_op | source)
XLA Modules:
  0.0 34.7 jit_solution(5779123415678956692)
XLA Ops:
  0.0 33.6 %shard_map.64 = f32[3,12,2,16,256]{4,3,2,1,0:T(8,128)S(1)} custom-call(s32[3]{0:T(128)} %shift_h.1, f32[3,12,2,16,256]{4,3,2,1,0:T(8,128)} %pos_h.1, f32[3,12,2,16,256]{4,3,2,1,0:T(8,128)} %vel_h.1, f32[3,12,2,16,256]{4,3,2,1,0:T(8,128)} %th_h.1, s32[12,2,16,256]{3,2,1,0:T(8,128)} %off_h.1, s32[12,2,16,256]{3,2,1,0:T(8,128)} %occ_h.1), custom_call_target="tpu_custom_call" | custom-call | tf_op jit(solution)/shard_map/pallas_call | solution.py:402
  33.7 1.0 %copy.8 = f32[3,12,2,16,256]{4,3,2,1,0:T(8,128)} copy(f32[3,12,2,16,256]{4,3,2,1,0:T(8,128)S(1)} %shard_map.64) | data formatting | bytes 2359296

commit v2 on v1

v2 whole, which is shorter than its diff:
```python
import functools

import jax
import jax.numpy as jnp
from jax import lax
from jax.experimental import pallas as pl
from jax.experimental.pallas import tpu as pltpu
from jax.sharding import PartitionSpec as P

STEPS = 3
RIDGE = 0.5
F32 = jnp.float32
NS = 10
ND = 6
DIRS = ((-1, 0), (1, 0), (0, -1), (0, 1), (-1, -1), (-1, 1), (1, -1), (1, 1))


def pad8(v):
    return (v + 7) // 8 * 8


def cross(a, b):
    return [
        a[1] * b[2] - a[2] * b[1],
        a[2] * b[0] - a[0] * b[2],
        a[0] * b[1] - a[1] * b[0],
    ]


def translate_static(m, axis):
    n, x, y, z, xx, yy, zz, xy, xz, yz = m
    if axis == 0:
        return [n, x + n, y, z, xx + (x + x) + n, yy, zz, xy + y, xz + z, yz]
    if axis == 1:
        return [n, x, y + n, z, xx, yy + (y + y) + n, zz, xy + x, xz, yz + z]
    return [n, x, y, z + n, xx, yy, zz + (z + z) + n, xy, xz + x, yz + y]


def translate_dynamic(m, axis):
    wx, wy, wz, lx, ly, lz = m
    if axis == 0:
        return [wx, wy, wz, lx, ly - wz, lz + wy]
    if axis == 1:
        return [wx, wy, wz, lx + wz, ly, lz - wx]
    return [wx, wy, wz, lx - wy, ly + wx, lz]


def kernel(
    shift_h, pos_h, vel_h, th_h, off_h, occ_h, res,
    shift_ref, pos, vel, th, off, occ, code, grp, upd, made, est, edy,
    sx_s, sy_s, sc_s, rx_s, ry_s, rc_s, sx_d, sy_d, sc_d, rx_d, ry_d, rc_d,
    in_sem, row_sem, send_sem, recv_sem,
):
    slots, rows, cols, depth = off.shape
    gx, gy = lax.axis_index("gx"), lax.axis_index("gy")
    nx, ny = lax.axis_size("gx"), lax.axis_size("gy")

    def device(dx, dy):
        return (lax.rem(gx + dx + nx, nx), lax.rem(gy + dy + ny, ny))

    shift_load = pltpu.make_async_copy(shift_h, shift_ref, in_sem.at[0])
    shift_load.start()
    lead = lax.rem(gx, 2)
    lead_row, lead_half, lead_edge = lead * (rows - 1), 1 - lead, lead * rows
    tail_row, tail_half, tail_edge = rows - 1 - lead_row, lead, rows - lead_edge
    loads = []
    for k, r in enumerate([lead_row, tail_row][: min(rows, 2)] + list(range(1, rows - 1))):
        pairs = (
            (off_h.at[:, r], off.at[:, r]),
            (occ_h.at[:, r], occ.at[:, r]),
            (pos_h.at[:, :, r], pos.at[:, :, r]),
            (th_h.at[:, :, r], th.at[:, :, r]),
            (vel_h.at[:, :, r], vel.at[:, :, r]),
        )
        loads.append(
            [pltpu.make_async_copy(a, b, row_sem.at[k, i]) for i, (a, b) in enumerate(pairs)]
        )
        for copy in loads[k]:
            copy.start()

    def wait_loads(wanted):
        for copy in wanted:
            copy.wait()

    barrier = pltpu.get_barrier_semaphore()
    for dx, dy in DIRS:
        pl.semaphore_signal(
            barrier, inc=1, device_id=device(dx, dy), device_id_type=pl.DeviceIdType.MESH
        )

    yb, zb = cols // 8, depth // 128
    blocks = yb * zb
    edges = [(0, 1), (rows - 1, 0)]
    second = [(r, h) for r in range(rows) for h in range(2) if (r, h) not in edges]

    def place(r, index):
        y = pl.multiple_of((index // zb) * 8, 8)
        z = pl.multiple_of((index % zb) * 128, 128)
        return r, pl.ds(y, 8), pl.ds(z, 128)

    def accumulate(at, base, wanted, make_terms, new=False):
        total = None
        for m in range(slots):
            if new:
                moved = jnp.bitwise_xor(off[(m,) + at], shift_ref[0])
                own = jnp.where(occ[(m,) + at] == 1, moved, 8)
                code[(m,) + at] = own
            else:
                own = code[(m,) + at]
            terms = make_terms(m)
            picked = []
            for c in wanted:
                mask = own == c
                picked.append([jnp.where(mask, t, 0.0) for t in terms])
            if total is None:
                total = picked
            else:
                total = [[a + b for a, b in zip(u, v)] for u, v in zip(total, picked)]
        for c, values in zip(wanted, total):
            for k, value in enumerate(values):
                grp[(base + k, c) + at] = value

    def point(m, at):
        return [pos[(k, m) + at] for k in range(3)]

    def codes_of(h):
        return [4 * h + c for c in range(4)]

    def shifted(s):
        return jnp.bitwise_xor(shift_ref[s], shift_ref[0])

    def static_sums(r, h, new=False):
        def body(index, carry):
            at = place(r, index)

            def terms(m):
                x, y, z = point(m, at)
                return [1.0, x, y, z, x * x, y * y, z * z, x * y, x * z, y * z]

            accumulate(at, 0, codes_of(h), terms, new)
            return carry

        lax.fori_loop(0, blocks, body, 0)

    def flow_sums(step, r, wanted):
        def body(index, carry):
            at = place(r, index)

            def terms(m):
                now = [th[(k, (m + step) % slots) + at] for k in range(3)]
                if step == 0:
                    before = [vel[(k, m) + at] for k in range(3)]
                else:
                    before = [th[(k, (m + step - 1) % slots) + at] for k in range(3)]
                flow = [a - b for a, b in zip(before, now)]
                return flow + cross(point(m, at), flow)

            accumulate(at, NS + ND * step, wanted, terms)
            return carry

        lax.fori_loop(0, blocks, body, 0)

    sub = lax.broadcasted_iota(jnp.int32, (cols, depth), 0)

    def build(load, translate, count, ext, sx, sy, sc, edges):
        def merged(e, by):
            halves = []
            for bz in range(2):
                parts = []
                if e > 0:
                    parts.append(load(2 * by + bz, e - 1))
                if e < rows:
                    parts.append(translate(load(4 + 2 * by + bz, e), 0))
                halves.append(parts[0] if len(parts) == 1 else [a + b for a, b in zip(*parts)])
            high = [pltpu.roll(v, depth - 1, 1) for v in translate(halves[1], 2)]
            return [a + b for a, b in zip(halves[0], high)]

        for e in edges:
            low = merged(e, 0)
            high = translate(merged(e, 1), 1)
            for v in range(count):
                moved = pltpu.roll(high[v], cols - 1, 0)
                main = low[v] + jnp.where(sub == cols - 1, 0.0, moved)
                rim, last = high[v][0:1], main[cols - 1 : cols]
                ext[v, e, 0:cols] = main
                ext[v, e, cols : cols + 1] = rim
                for side, row in ((0, 0), (1, rows)):
                    if e == row:
                        sx[side, v * cols : (v + 1) * cols] = main
                        sx[side, count * cols + v : count * cols + v + 1] = rim
                        sc[2 * side, v : v + 1] = rim
                        sc[2 * side + 1, v : v + 1] = last
                sy[0, e * count + v : e * count + v + 1] = rim
                sy[1, e * count + v : e * count + v + 1] = last

    def copies(sx, sy, sc, rx, ry, rc, kind, step):
        out = []
        for k, (dx, dy) in enumerate(DIRS):
            if dy == 0:
                src, dst = sx.at[k], rx.at[k]
            elif dx == 0:
                src, dst = sy.at[k - 2], ry.at[k - 2]
            else:
                src, dst = sc.at[k - 4], rc.at[k - 4]
            out.append(
                pltpu.make_async_remote_copy(
                    src_ref=src, dst_ref=dst,
                    send_sem=send_sem.at[kind, step, k],
                    recv_sem=recv_sem.at[kind, step, k],
                    device_id=device(dx, dy),
                    device_id_type=pl.DeviceIdType.MESH,
                )
            )
        return out

    def absorb(count, ext, rx, ry, rc, sent):
        for copy in sent:
            copy.wait_recv()
        for v in range(count):
            for side, e in ((0, rows), (1, 0)):
                ext[v, e, 0:cols] += rx[side, v * cols : (v + 1) * cols]
                ext[v, e, cols : cols + 1] += rx[side, count * cols + v : count * cols + v + 1]
            for e in range(rows + 1):
                for side, row in ((0, cols - 1), (1, cols)):
                    extra = ry[side, e * count + v : e * count + v + 1]
                    if e == rows:
                        extra = extra + rc[side, v : v + 1]
                    if e == 0:
                        extra = extra + rc[2 + side, v : v + 1]
                    ext[v, e, row : row + 1] += extra

    def static_solve(ext):
        for e in range(rows + 1):
            n, sx, sy, sz, xx, yy, zz, xy, xz, yz = [ext[v, e] for v in range(NS)]
            inv = 1.0 / jnp.maximum(n, 1.0)
            cx, cy, cz = sx * inv, sy * inv, sz * inv
            mxx, myy, mzz = xx - sx * cx, yy - sy * cy, zz - sz * cz
            kxy, kxz, kyz = sx * cy - xy, sx * cz - xz, sy * cz - yz
            kxx = myy + mzz + RIDGE
            kyy = mxx + mzz + RIDGE
            kzz = mxx + myy + RIDGE
            axx = kyy * kzz - kyz * kyz
            ayy = kxx * kzz - kxz * kxz
            azz = kxx * kyy - kxy * kxy
            axy = kxz * kyz - kxy * kzz
            axz = kxy * kyz - kxz * kyy
            ayz = kxy * kxz - kxx * kyz
            scale = 1.0 / (kxx * axx + kxy * axy + kxz * axz)
            done = [inv, cx, cy, cz] + [a * scale for a in (axx, ayy, azz, axy, axz, ayz)]
            for v in range(NS):
                ext[v, e] = done[v]

    def table(ext, dyn, e):
        inv, cx, cy, cz, ixx, iyy, izz, ixy, ixz, iyz = [ext[v, e] for v in range(NS)]
        flow = [dyn[v, e] for v in range(3)]
        centre = [cx, cy, cz]
        tq = [dyn[3 + k, e] - t for k, t in enumerate(cross(centre, flow))]
        spin = [
            ixx * tq[0] + ixy * tq[1] + ixz * tq[2],
            ixy * tq[0] + iyy * tq[1] + iyz * tq[2],
            ixz * tq[0] + iyz * tq[1] + izz * tq[2],
        ]
        base = [f * inv - t for f, t in zip(flow, cross(spin, centre))]
        values = base + spin
        straight = [v[0:cols] for v in values]
        moved = [
            jnp.where(
                sub == 0,
                jnp.broadcast_to(v[cols : cols + 1], (cols, depth)),
                pltpu.roll(v[0:cols], 1, 0),
            )
            for v in values
        ]
        for by, plain in ((0, straight), (1, moved)):
            for v in range(ND):
                made[e, by, 0, v] = plain[v]
                made[e, by, 1, v] = pltpu.roll(plain[v], 1, 1)

    def solve_row(step, r):
        delta = shifted(step)
        for want in range(8):
            bits = (want // 4, want // 2 % 2, want % 2)
            a0, a1, a2, s0, s1, s2 = [
                made[r - bits[0] + 1, bits[1], bits[2], v] for v in range(ND)
            ]
            if bits[2]:
                a0, a1 = a0 + s1, a1 - s0
            if bits[1]:
                a0, a2 = a0 - s2, a2 + s0
            if bits[0]:
                a1, a2 = a1 + s2, a2 - s1
            if step == STEPS - 1:
                done = [a0, a1, a2, s0, s1, s2]
            else:
                own = jnp.bitwise_xor(delta, want)
                n, x, y, z, xx, yy, zz, xy, xz, yz = [grp[v, own, r] for v in range(NS)]
                turn = cross([s0, s1, s2], [x, y, z])
                arm = cross([x, y, z], [a0, a1, a2])
                done = [
                    n * a0 + turn[0],
                    n * a1 + turn[1],
                    n * a2 + turn[2],
                    arm[0] + (yy + zz) * s0 - xy * s1 - xz * s2,
                    arm[1] + (xx + zz) * s1 - xy * s0 - yz * s2,
                    arm[2] + (xx + yy) * s2 - xz * s0 - yz * s1,
                ]
            for v in range(ND):
                upd[v, want, r] = done[v]

    def load_static(step):
        delta = shifted(step)

        def load(want, r):
            own = want if step == 0 else jnp.bitwise_xor(delta, want)
            return [grp[v, own, r] for v in range(NS)]

        return load

    def load_dynamic(step):
        delta = shifted(step)

        def load(want, r):
            own = want if step == 0 else jnp.bitwise_xor(delta, want)
            values = [grp[NS + ND * step + v, own, r] for v in range(ND)]
            if step:
                last = jnp.bitwise_xor(own, shifted(step - 1))
                values = [a + upd[v, last, r] for v, a in enumerate(values)]
            return values

        return load

    static_sent = [
        copies(sx_s.at[s], sy_s.at[s], sc_s.at[s], rx_s.at[s], ry_s.at[s], rc_s.at[s], 0, s)
        for s in range(STEPS)
    ]
    dynamic_sent = [
        copies(sx_d.at[s], sy_d.at[s], sc_d.at[s], rx_d.at[s], ry_d.at[s], rc_d.at[s], 1, s)
        for s in range(STEPS)
    ]
    groups = {0: (0, 4, 5), rows: (1, 6, 7)}

    def send_edge(sent, e):
        for k in groups[e]:
            sent[k].start()

    def send_sides(sent):
        sent[2].start()
        sent[3].start()

    def build_static(s, edges):
        build(
            load_static(s), translate_static, NS, est.at[s],
            sx_s.at[s], sy_s.at[s], sc_s.at[s], edges,
        )

    def build_dynamic(s, edges):
        build(
            load_dynamic(s), translate_dynamic, ND, edy,
            sx_d.at[s], sy_d.at[s], sc_d.at[s], edges,
        )

    def send_static(s):
        for e in (0, rows):
            send_edge(static_sent[s], e)
        send_sides(static_sent[s])

    def finish_static(s):
        absorb(NS, est.at[s], rx_s.at[s], ry_s.at[s], rc_s.at[s], static_sent[s])
        static_solve(est.at[s])

    inner = range(1, rows)

    def at_edge(edge, act):
        for e in (0, rows):
            pl.when(edge == e)(functools.partial(act, e))

    def static_edge(s, e):
        build_static(s, [e])
        send_edge(static_sent[s], e)

    def dynamic_edge(s, e):
        build_dynamic(s, [e])
        send_edge(dynamic_sent[s], e)

    shift_load.wait()
    wait_loads(loads[0][:3])
    static_sums(lead_row, lead_half, True)
    pl.semaphore_wait(barrier, len(DIRS))
    at_edge(lead_edge, functools.partial(static_edge, 0))
    wait_loads(loads[0][3:])
    flow_sums(0, lead_row, codes_of(lead_half))
    at_edge(lead_edge, functools.partial(dynamic_edge, 0))
    for group in loads[1:]:
        wait_loads(group)
    static_sums(tail_row, tail_half, True)
    at_edge(tail_edge, functools.partial(static_edge, 0))
    flow_sums(0, tail_row, codes_of(tail_half))
    at_edge(tail_edge, functools.partial(dynamic_edge, 0))
    for r, h in second:
        static_sums(r, h, 0 < r < rows - 1 and h == 0)
    build_static(0, inner)
    send_sides(static_sent[0])
    for r, h in second:
        flow_sums(0, r, codes_of(h))
    build_dynamic(0, inner)
    send_sides(dynamic_sent[0])
    build_static(1, range(rows + 1))
    send_static(1)
    for r in range(rows):
        flow_sums(1, r, range(8))
    finish_static(0)
    for s in range(STEPS):
        absorb(ND, edy, rx_d.at[s], ry_d.at[s], rc_d.at[s], dynamic_sent[s])
        table(est.at[s], edy, lead_edge)
        for e in inner:
            table(est.at[s], edy, e)
        solve_row(s, lead_row)
        if s + 1 < STEPS:
            at_edge(lead_edge, functools.partial(dynamic_edge, s + 1))
        table(est.at[s], edy, tail_edge)
        if rows > 1:
            solve_row(s, tail_row)
        if s + 1 < STEPS:
            at_edge(tail_edge, functools.partial(dynamic_edge, s + 1))
        for r in range(1, rows - 1):
            solve_row(s, r)
        if s + 1 < STEPS:
            build_dynamic(s + 1, inner)
            send_sides(dynamic_sent[s + 1])
            if s == 0:
                build_static(2, range(rows + 1))
                for r in range(rows):
                    flow_sums(2, r, range(8))
                send_static(2)
            finish_static(s + 1)

    last_delta = shifted(STEPS - 1)
    last_step = STEPS - 1

    def final_block(r, index, carry):
        at = place(r, index)
        for start in range(0, slots, 6):
            batch = range(start, min(start + 6, slots))
            codes = {m: code[(m,) + at] for m in batch}
            picked = {m: [] for m in batch}
            for v in range(ND):
                leaf = [upd[(v, jnp.bitwise_xor(last_delta, o)) + at] for o in range(8)]
                for m in batch:
                    one = jnp.bitwise_and(codes[m], 1) == 1
                    two = jnp.bitwise_and(codes[m], 2) == 2
                    four = jnp.bitwise_and(codes[m], 4) == 4
                    level = [jnp.where(one, leaf[k + 1], leaf[k]) for k in range(0, 8, 2)]
                    level = [jnp.where(two, level[k + 1], level[k]) for k in range(0, 4, 2)]
                    picked[m].append(jnp.where(four, level[1], level[0]))
            for m in batch:
                turn = cross(picked[m][3:], point(m, at))
                full = codes[m] < 8
                for k in range(3):
                    hot = th[(k, (m + last_step) % slots) + at]
                    res[(k, m) + at] = jnp.where(full, hot + picked[m][k] + turn[k], 0.0)
        return carry

    for r in range(rows):
        lax.fori_loop(0, blocks, functools.partial(final_block, r), 0)
    for group in static_sent + dynamic_sent:
        for copy in group:
            copy.wait_send()


def local(positions, velocities, thermal, offsets, occupancy, shift_codes):
    args = (shift_codes, positions, velocities, thermal, offsets, occupancy)
    slots, rows, cols, depth = offsets.shape
    full = (3, slots, rows, cols, depth)
    plane = (slots, rows, cols, depth)

    def faces(count):
        wide = pltpu.VMEM((STEPS, 2, count * cols + pad8(count), depth), F32)
        thin = pltpu.VMEM((STEPS, 2, pad8((rows + 1) * count), depth), F32)
        tips = pltpu.VMEM((STEPS, 4, pad8(count), depth), F32)
        return [wide, thin, tips] * 2

    hbm = pl.BlockSpec(memory_space=pltpu.HBM)
    return pl.pallas_call(
        kernel,
        out_shape=pltpu.VMEM(full, F32),
        in_specs=[hbm] * 6,
        out_specs=pl.BlockSpec(memory_space=pltpu.VMEM),
        scratch_shapes=[
            pltpu.SMEM((STEPS,), jnp.int32),
            pltpu.VMEM(full, F32),
            pltpu.VMEM(full, F32),
            pltpu.VMEM(full, F32),
            pltpu.VMEM(plane, jnp.int32),
            pltpu.VMEM(plane, jnp.int32),
            pltpu.VMEM(plane, jnp.int32),
            pltpu.VMEM((NS + ND * STEPS, 8, rows, cols, depth), F32),
            pltpu.VMEM((ND, 8, rows, cols, depth), F32),
            pltpu.VMEM((rows + 1, 2, 2, ND, cols, depth), F32),
            pltpu.VMEM((STEPS, NS, rows + 1, cols + 8, depth), F32),
            pltpu.VMEM((ND, rows + 1, cols + 8, depth), F32),
            *faces(NS),
            *faces(ND),
            pltpu.SemaphoreType.DMA((1,)),
            pltpu.SemaphoreType.DMA((rows, 5)),
            pltpu.SemaphoreType.DMA((2, STEPS, len(DIRS))),
            pltpu.SemaphoreType.DMA((2, STEPS, len(DIRS))),
        ],
        compiler_params=pltpu.CompilerParams(
            collective_id=0, has_side_effects=True, vmem_limit_bytes=40000000
        ),
    )(*[pltpu.with_memory_space_constraint(v, pltpu.HBM) for v in args])


def solution(mesh):
    in_specs = (
        P(None, None, "gx", "gy", None),
        P(None, None, "gx", "gy", None),
        P(None, None, "gx", "gy", None),
        P(None, "gx", "gy", None),
        P(None, "gx", "gy", None),
        P(),
    )
    out_specs = P(None, None, "gx", "gy", None)
    return jax.shard_map(local, mesh=mesh, in_specs=in_specs, out_specs=out_specs, check_vma=False)
```

time: 34.8 us -> 32.7 us (0.940)
  Pallas kernels: 33.6 us -> 31.4 us
    pallas_call x1, Pallas kernels: 33.6 us -> 31.4 us  [local(): pl.pallas_call(kernel, out_shape=pltpu.VMEM(full, F32), in_specs=[hbm] *...]
where the time goes in v2:
time: 32.7 us; the launch traced here: 32.4 us
  Pallas kernels  31.4 us (96%)
  local copies, waits for them, and re-layouts  1.02 us (3%)
    pallas_call x1, Pallas kernels, local(): pl.pallas_call(kernel, out_shape=pltpu.VMEM(full, F32), in_specs=[hbm] *...  31.4 us
    unnamed x1, local copies, waits for them, and re-layouts  1.02 us

profile of v2, /device:TPU:1, one launch (start us, length us, event | category | flops | bytes accessed | tf_op | source)
XLA Modules:
  0.0 32.4 jit_solution(9473579704670655505)
XLA Ops:
  0.0 31.4 %shard_map.64 = f32[3,12,2,16,256]{4,3,2,1,0:T(8,128)S(1)} custom-call(s32[3]{0:T(128)} %shift_h.1, f32[3,12,2,16,256]{4,3,2,1,0:T(8,128)} %pos_h.1, f32[3,12,2,16,256]{4,3,2,1,0:T(8,128)} %vel_h.1, f32[3,12,2,16,256]{4,3,2,1,0:T(8,128)} %th_h.1, s32[12,2,16,256]{3,2,1,0:T(8,128)} %off_h.1, s32[12,2,16,256]{3,2,1,0:T(8,128)} %occ_h.1), custom_call_target="tpu_custom_call" | custom-call | tf_op jit(solution)/shard_map/pallas_call | solution.py:483
  31.4 1.0 %copy.8 = f32[3,12,2,16,256]{4,3,2,1,0:T(8,128)} copy(f32[3,12,2,16,256]{4,3,2,1,0:T(8,128)S(1)} %shard_map.64) | data formatting | bytes 2359296

commit v3 on v2

--- a/solution.py
+++ b/solution.py
@@ -188,14 +188,15 @@
                     if e == row:
                         sx[side, v * cols : (v + 1) * cols] = main
                         sx[side, count * cols + v : count * cols + v + 1] = rim
-                        sc[2 * side, v : v + 1] = rim
-                        sc[2 * side + 1, v : v + 1] = last
+                        if sc is not None:
+                            sc[2 * side, v : v + 1] = rim
+                            sc[2 * side + 1, v : v + 1] = last
                 sy[0, e * count + v : e * count + v + 1] = rim
                 sy[1, e * count + v : e * count + v + 1] = last
 
     def copies(sx, sy, sc, rx, ry, rc, kind, step):
         out = []
-        for k, (dx, dy) in enumerate(DIRS):
+        for k, (dx, dy) in enumerate(DIRS if sc is not None else DIRS[:4]):
             if dy == 0:
                 src, dst = sx.at[k], rx.at[k]
             elif dx == 0:
@@ -213,21 +214,33 @@
             )
         return out
 
-    def absorb(count, ext, rx, ry, rc, sent):
+    def absorb_sides(count, ext, ry, rc, sx, sent, wanted):
+        for copy in sent:
+            copy.wait_recv()
+        for v in range(count):
+            for e in wanted:
+                for side, row in ((0, cols - 1), (1, cols)):
+                    extra = ry[side, e * count + v : e * count + v + 1]
+                    if rc is not None and e == rows:
+                        extra = extra + rc[side, v : v + 1]
+                    if rc is not None and e == 0:
+                        extra = extra + rc[2 + side, v : v + 1]
+                    ext[v, e, row : row + 1] += extra
+                if sx is not None and e in (0, rows):
+                    for side, edge in ((0, 0), (1, rows)):
+                        if e == edge:
+                            at = v * cols + cols - 1
+                            sx[side, at : at + 1] = ext[v, e, cols - 1 : cols]
+                            at = count * cols + v
+                            sx[side, at : at + 1] = ext[v, e, cols : cols + 1]
+
+    def absorb_edges(count, ext, rx, sent):
         for copy in sent:
             copy.wait_recv()
         for v in range(count):
             for side, e in ((0, rows), (1, 0)):
                 ext[v, e, 0:cols] += rx[side, v * cols : (v + 1) * cols]
                 ext[v, e, cols : cols + 1] += rx[side, count * cols + v : count * cols + v + 1]
-            for e in range(rows + 1):
-                for side, row in ((0, cols - 1), (1, cols)):
-                    extra = ry[side, e * count + v : e * count + v + 1]
-                    if e == rows:
-                        extra = extra + rc[side, v : v + 1]
-                    if e == 0:
-                        extra = extra + rc[2 + side, v : v + 1]
-                    ext[v, e, row : row + 1] += extra
 
     def static_solve(ext):
         for e in range(rows + 1):
@@ -276,18 +289,19 @@
                 made[e, by, 0, v] = plain[v]
                 made[e, by, 1, v] = pltpu.roll(plain[v], 1, 1)
 
-    def solve_row(step, r):
+    def solve_half(step, r, h):
         delta = shifted(step)
-        for want in range(8):
-            bits = (want // 4, want // 2 % 2, want % 2)
-            a0, a1, a2, s0, s1, s2 = [
-                made[r - bits[0] + 1, bits[1], bits[2], v] for v in range(ND)
-            ]
-            if bits[2]:
+        for c in range(4):
+            want = 4 * h + c
+            a0, a1, a2, s0, s1, s2 = [made[r - h + 1, c // 2, c % 2, v] for v in range(ND)]
+            if c % 2:
                 a0, a1 = a0 + s1, a1 - s0
-            if bits[1]:
+            if c // 2:
                 a0, a2 = a0 - s2, a2 + s0
-            if bits[0]:
+            if not isinstance(h, int):
+                side = lax.convert_element_type(h, F32)
+                a1, a2 = a1 + side * s2, a2 - side * s1
+            elif h:
                 a1, a2 = a1 + s2, a2 - s1
             if step == STEPS - 1:
                 done = [a0, a1, a2, s0, s1, s2]
@@ -307,6 +321,35 @@
             for v in range(ND):
                 upd[v, want, r] = done[v]
 
+    last_step = STEPS - 1
+    written = set()
+
+    def final_half(r, h):
+        delta = shifted(last_step)
+        fresh = r not in written
+        written.add(r)
+
+        def body(index, carry):
+            at = place(r, index)
+            leaf = [[upd[(v, 4 * h + c) + at] for c in range(4)] for v in range(ND)]
+            for m in range(slots):
+                own = jnp.bitwise_xor(code[(m,) + at], delta)
+                one = jnp.bitwise_and(own, 1) == 1
+                two = jnp.bitwise_and(own, 2) == 2
+                mine = jnp.bitwise_and(own, 12) == 4 * h
+                picked = [
+                    jnp.where(two, jnp.where(one, l[3], l[2]), jnp.where(one, l[1], l[0]))
+                    for l in leaf
+                ]
+                turn = cross(picked[3:], point(m, at))
+                for k in range(3):
+                    hot = th[(k, (m + last_step) % slots) + at]
+                    old = 0.0 if fresh else res[(k, m) + at]
+                    res[(k, m) + at] = jnp.where(mine, hot + picked[k] + turn[k], old)
+            return carry
+
+        lax.fori_loop(0, blocks, body, 0)
+
     def load_static(step):
         delta = shifted(step)
 
@@ -329,8 +372,9 @@
 
         return load
 
+    tips = [(sc_s.at[s], rc_s.at[s]) if s + 1 < STEPS else (None, None) for s in range(STEPS)]
     static_sent = [
-        copies(sx_s.at[s], sy_s.at[s], sc_s.at[s], rx_s.at[s], ry_s.at[s], rc_s.at[s], 0, s)
+        copies(sx_s.at[s], sy_s.at[s], tips[s][0], rx_s.at[s], ry_s.at[s], tips[s][1], 0, s)
         for s in range(STEPS)
     ]
     dynamic_sent = [
@@ -341,7 +385,8 @@
 
     def send_edge(sent, e):
         for k in groups[e]:
-            sent[k].start()
+            if k < len(sent):
+                sent[k].start()
 
     def send_sides(sent):
         sent[2].start()
@@ -350,7 +395,7 @@
     def build_static(s, edges):
         build(
             load_static(s), translate_static, NS, est.at[s],
-            sx_s.at[s], sy_s.at[s], sc_s.at[s], edges,
+            sx_s.at[s], sy_s.at[s], tips[s][0], edges,
         )
 
     def build_dynamic(s, edges):
@@ -359,16 +404,34 @@
             sx_d.at[s], sy_d.at[s], sc_d.at[s], edges,
         )
 
+    inner, every = range(1, rows), range(rows + 1)
+
+    def begin_static(s):
+        build_static(s, every)
+        send_sides(static_sent[s])
+
     def send_static(s):
+        if tips[s][1] is None:
+            absorb_sides(NS, est.at[s], ry_s.at[s], None, sx_s.at[s], static_sent[s][2:], every)
         for e in (0, rows):
             send_edge(static_sent[s], e)
-        send_sides(static_sent[s])
 
     def finish_static(s):
-        absorb(NS, est.at[s], rx_s.at[s], ry_s.at[s], rc_s.at[s], static_sent[s])
+        absorb_edges(NS, est.at[s], rx_s.at[s], static_sent[s][:2])
+        if tips[s][1] is not None:
+            absorb_sides(
+                NS, est.at[s], ry_s.at[s], tips[s][1], None, static_sent[s][2:], every
+            )
         static_solve(est.at[s])
 
-    inner = range(1, rows)
+    def absorb_inner(s):
+        sent = dynamic_sent[s][2:4]
+        absorb_sides(ND, edy, ry_d.at[s], None, None, sent, inner)
+
+    def absorb_outer(s):
+        sent = dynamic_sent[s]
+        absorb_edges(ND, edy, rx_d.at[s], sent[:2])
+        absorb_sides(ND, edy, ry_d.at[s], rc_d.at[s], None, sent[4:], (0, rows))
 
     def at_edge(edge, act):
         for e in (0, rows):
@@ -404,64 +467,41 @@
         flow_sums(0, r, codes_of(h))
     build_dynamic(0, inner)
     send_sides(dynamic_sent[0])
-    build_static(1, range(rows + 1))
-    send_static(1)
+    begin_static(1)
     for r in range(rows):
         flow_sums(1, r, range(8))
+        if r == 0:
+            send_static(1)
+    begin_static(2)
     finish_static(0)
     for s in range(STEPS):
-        absorb(ND, edy, rx_d.at[s], ry_d.at[s], rc_d.at[s], dynamic_sent[s])
-        table(est.at[s], edy, lead_edge)
+        absorb_inner(s)
         for e in inner:
             table(est.at[s], edy, e)
-        solve_row(s, lead_row)
-        if s + 1 < STEPS:
+        for r, h in second:
+            solve_half(s, r, h)
+        if s == last_step:
+            for r, h in second:
+                final_half(r, h)
+        absorb_outer(s)
+        table(est.at[s], edy, lead_edge)
+        solve_half(s, lead_row, lead_half)
+        if s < last_step:
             at_edge(lead_edge, functools.partial(dynamic_edge, s + 1))
         table(est.at[s], edy, tail_edge)
-        if rows > 1:
-            solve_row(s, tail_row)
-        if s + 1 < STEPS:
+        solve_half(s, tail_row, tail_half)
+        if s < last_step:
             at_edge(tail_edge, functools.partial(dynamic_edge, s + 1))
-        for r in range(1, rows - 1):
-            solve_row(s, r)
-        if s + 1 < STEPS:
             build_dynamic(s + 1, inner)
             send_sides(dynamic_sent[s + 1])
             if s == 0:
-                build_static(2, range(rows + 1))
                 for r in range(rows):
                     flow_sums(2, r, range(8))
-                send_static(2)
+                    if r == 0:
+                        send_static(2)
             finish_static(s + 1)
-
-    last_delta = shifted(STEPS - 1)
-    last_step = STEPS - 1
-
-    def final_block(r, index, carry):
-        at = place(r, index)
-        for start in range(0, slots, 6):
-            batch = range(start, min(start + 6, slots))
-            codes = {m: code[(m,) + at] for m in batch}
-            picked = {m: [] for m in batch}
-            for v in range(ND):
-                leaf = [upd[(v, jnp.bitwise_xor(last_delta, o)) + at] for o in range(8)]
-                for m in batch:
-                    one = jnp.bitwise_and(codes[m], 1) == 1
-                    two = jnp.bitwise_and(codes[m], 2) == 2
-                    four = jnp.bitwise_and(codes[m], 4) == 4
-                    level = [jnp.where(one, leaf[k + 1], leaf[k]) for k in range(0, 8, 2)]
-                    level = [jnp.where(two, level[k + 1], level[k]) for k in range(0, 4, 2)]
-                    picked[m].append(jnp.where(four, level[1], level[0]))
-            for m in batch:
-                turn = cross(picked[m][3:], point(m, at))
-                full = codes[m] < 8
-                for k in range(3):
-                    hot = th[(k, (m + last_step) % slots) + at]
-                    res[(k, m) + at] = jnp.where(full, hot + picked[m][k] + turn[k], 0.0)
-        return carry
-
-    for r in range(rows):
-        lax.fori_loop(0, blocks, functools.partial(final_block, r), 0)
+    for r, h in edges:
+        final_half(r, h)
     for group in static_sent + dynamic_sent:
         for copy in group:
             copy.wait_send()
@@ -473,10 +513,10 @@
     full = (3, slots, rows, cols, depth)
     plane = (slots, rows, cols, depth)
 
-    def faces(count):
+    def faces(count, tip_steps):
         wide = pltpu.VMEM((STEPS, 2, count * cols + pad8(count), depth), F32)
         thin = pltpu.VMEM((STEPS, 2, pad8((rows + 1) * count), depth), F32)
-        tips = pltpu.VMEM((STEPS, 4, pad8(count), depth), F32)
+        tips = pltpu.VMEM((tip_steps, 4, pad8(count), depth), F32)
         return [wide, thin, tips] * 2
 
     hbm = pl.BlockSpec(memory_space=pltpu.HBM)
@@ -498,8 +538,8 @@
             pltpu.VMEM((rows + 1, 2, 2, ND, cols, depth), F32),
             pltpu.VMEM((STEPS, NS, rows + 1, cols + 8, depth), F32),
             pltpu.VMEM((ND, rows + 1, cols + 8, depth), F32),
-            *faces(NS),
-            *faces(ND),
+            *faces(NS, STEPS - 1),
+            *faces(ND, STEPS),
             pltpu.SemaphoreType.DMA((1,)),
             pltpu.SemaphoreType.DMA((rows, 5)),
             pltpu.SemaphoreType.DMA((2, STEPS, len(DIRS))),

time: 32.7 us -> 31.2 us (0.954)
  Pallas kernels: 31.4 us -> 30 us
    pallas_call x1, Pallas kernels: 31.4 us -> 30 us  [local(): pl.pallas_call(kernel, out_shape=pltpu.VMEM(full, F32), in_specs=[hbm] *...]
where the time goes in v3:
time: 31.2 us; the launch traced here: 31 us
  Pallas kernels  30 us (96%)
  local copies, waits for them, and re-layouts  1.02 us (3%)
    pallas_call x1, Pallas kernels, local(): pl.pallas_call(kernel, out_shape=pltpu.VMEM(full, F32), in_specs=[hbm] *...  30 us
    unnamed x1, local copies, waits for them, and re-layouts  1.02 us

profile of v3, /device:TPU:1, one launch (start us, length us, event | category | flops | bytes accessed | tf_op | source)
XLA Modules:
  0.0 31.0 jit_solution(6736978620627102486)
XLA Ops:
  0.0 30.0 %shard_map.64 = f32[3,12,2,16,256]{4,3,2,1,0:T(8,128)S(1)} custom-call(s32[3]{0:T(128)} %shift_h.1, f32[3,12,2,16,256]{4,3,2,1,0:T(8,128)} %pos_h.1, f32[3,12,2,16,256]{4,3,2,1,0:T(8,128)} %vel_h.1, f32[3,12,2,16,256]{4,3,2,1,0:T(8,128)} %th_h.1, s32[12,2,16,256]{3,2,1,0:T(8,128)} %off_h.1, s32[12,2,16,256]{3,2,1,0:T(8,128)} %occ_h.1), custom_call_target="tpu_custom_call" | custom-call | tf_op jit(solution)/shard_map/pallas_call | solution.py:523
  30.0 1.0 %copy.8 = f32[3,12,2,16,256]{4,3,2,1,0:T(8,128)} copy(f32[3,12,2,16,256]{4,3,2,1,0:T(8,128)S(1)} %shard_map.64) | data formatting | bytes 2359296

commit v4 on v3

--- a/solution.py
+++ b/solution.py
@@ -48,7 +48,8 @@
 def kernel(
     shift_h, pos_h, vel_h, th_h, off_h, occ_h, res,
     shift_ref, pos, vel, th, off, occ, code, grp, upd, made, est, edy,
-    sx_s, sy_s, sc_s, rx_s, ry_s, rc_s, sx_d, sy_d, sc_d, rx_d, ry_d, rc_d,
+    sx_s, sy_s, sc_s, sr_s, rx_s, ry_s, rc_s, rr_s,
+    sx_d, sy_d, sc_d, sr_d, rx_d, ry_d, rc_d, rr_d,
     in_sem, row_sem, send_sem, recv_sem,
 ):
     slots, rows, cols, depth = off.shape
@@ -63,15 +64,21 @@
     lead = lax.rem(gx, 2)
     lead_row, lead_half, lead_edge = lead * (rows - 1), 1 - lead, lead * rows
     tail_row, tail_half, tail_edge = rows - 1 - lead_row, lead, rows - lead_edge
+    yb, zb = cols // 8, depth // 128
     loads = []
     for k, r in enumerate([lead_row, tail_row][: min(rows, 2)] + list(range(1, rows - 1))):
-        pairs = (
-            (off_h.at[:, r], off.at[:, r]),
-            (occ_h.at[:, r], occ.at[:, r]),
-            (pos_h.at[:, :, r], pos.at[:, :, r]),
+        pairs = []
+        for j in range(yb):
+            y = pl.ds(8 * j, 8)
+            pairs += [
+                (off_h.at[:, r, y], off.at[:, r, y]),
+                (occ_h.at[:, r, y], occ.at[:, r, y]),
+                (pos_h.at[:, :, r, y], pos.at[:, :, r, y]),
+            ]
+        pairs += [
             (th_h.at[:, :, r], th.at[:, :, r]),
             (vel_h.at[:, :, r], vel.at[:, :, r]),
-        )
+        ]
         loads.append(
             [pltpu.make_async_copy(a, b, row_sem.at[k, i]) for i, (a, b) in enumerate(pairs)]
         )
@@ -88,7 +95,6 @@
             barrier, inc=1, device_id=device(dx, dy), device_id_type=pl.DeviceIdType.MESH
         )
 
-    yb, zb = cols // 8, depth // 128
     blocks = yb * zb
     edges = [(0, 1), (rows - 1, 0)]
     second = [(r, h) for r in range(rows) for h in range(2) if (r, h) not in edges]
@@ -129,7 +135,7 @@
     def shifted(s):
         return jnp.bitwise_xor(shift_ref[s], shift_ref[0])
 
-    def static_sums(r, h, new=False):
+    def static_sums(r, h, new=False, start=0, stop=blocks):
         def body(index, carry):
             at = place(r, index)
 
@@ -140,7 +146,7 @@
             accumulate(at, 0, codes_of(h), terms, new)
             return carry
 
-        lax.fori_loop(0, blocks, body, 0)
+        lax.fori_loop(start, stop, body, 0)
 
     def flow_sums(step, r, wanted):
         def body(index, carry):
@@ -162,7 +168,17 @@
 
     sub = lax.broadcasted_iota(jnp.int32, (cols, depth), 0)
 
-    def build(load, translate, count, ext, sx, sy, sc, edges):
+    def put(ref, side, v, row):
+        for z in range(zb):
+            ref[side, v * zb + z : v * zb + z + 1] = row[:, z * 128 : (z + 1) * 128]
+
+    def add(ext, v, e, row, ref, side):
+        for z in range(zb):
+            ext[v, e, row : row + 1, z * 128 : (z + 1) * 128] += ref[
+                side, v * zb + z : v * zb + z + 1
+            ]
+
+    def build(load, translate, count, ext, sx, sy, sc, sr, edges):
         def merged(e, by):
             halves = []
             for bz in range(2):
@@ -187,60 +203,58 @@
                 for side, row in ((0, 0), (1, rows)):
                     if e == row:
                         sx[side, v * cols : (v + 1) * cols] = main
-                        sx[side, count * cols + v : count * cols + v + 1] = rim
+                        put(sr, side, v, rim)
                         if sc is not None:
-                            sc[2 * side, v : v + 1] = rim
-                            sc[2 * side + 1, v : v + 1] = last
+                            put(sc, 2 * side, v, rim)
+                            put(sc, 2 * side + 1, v, last)
                 sy[0, e * count + v : e * count + v + 1] = rim
                 sy[1, e * count + v : e * count + v + 1] = last
 
-    def copies(sx, sy, sc, rx, ry, rc, kind, step):
-        out = []
-        for k, (dx, dy) in enumerate(DIRS if sc is not None else DIRS[:4]):
-            if dy == 0:
-                src, dst = sx.at[k], rx.at[k]
-            elif dx == 0:
-                src, dst = sy.at[k - 2], ry.at[k - 2]
-            else:
-                src, dst = sc.at[k - 4], rc.at[k - 4]
-            out.append(
-                pltpu.make_async_remote_copy(
-                    src_ref=src, dst_ref=dst,
-                    send_sem=send_sem.at[kind, step, k],
-                    recv_sem=recv_sem.at[kind, step, k],
-                    device_id=device(dx, dy),
-                    device_id_type=pl.DeviceIdType.MESH,
-                )
+    def copies(sx, sy, sc, sr, rx, ry, rc, rr, kind, step):
+        moves = []
+        for k, where in enumerate(DIRS[:4]):
+            wide = k < 2
+            moves.append((where, sx.at[k] if wide else sy.at[k - 2], rx.at[k] if wide else ry.at[k - 2]))
+        for k, where in enumerate(DIRS[:2]):
+            moves.append((where, sr.at[k], rr.at[k]))
+        if sc is not None:
+            for k, where in enumerate(DIRS[4:]):
+                moves.append((where, sc.at[k], rc.at[k]))
+        return [
+            pltpu.make_async_remote_copy(
+                src_ref=src, dst_ref=dst,
+                send_sem=send_sem.at[kind, step, k],
+                recv_sem=recv_sem.at[kind, step, k],
+                device_id=device(*where),
+                device_id_type=pl.DeviceIdType.MESH,
             )
-        return out
-
-    def absorb_sides(count, ext, ry, rc, sx, sent, wanted):
+            for k, (where, src, dst) in enumerate(moves)
+        ]
+
+    def absorb_sides(count, ext, ry, rc, out, sent, wanted):
         for copy in sent:
             copy.wait_recv()
         for v in range(count):
             for e in wanted:
                 for side, row in ((0, cols - 1), (1, cols)):
-                    extra = ry[side, e * count + v : e * count + v + 1]
+                    ext[v, e, row : row + 1] += ry[side, e * count + v : e * count + v + 1]
                     if rc is not None and e == rows:
-                        extra = extra + rc[side, v : v + 1]
+                        add(ext, v, e, row, rc, side)
                     if rc is not None and e == 0:
-                        extra = extra + rc[2 + side, v : v + 1]
-                    ext[v, e, row : row + 1] += extra
-                if sx is not None and e in (0, rows):
-                    for side, edge in ((0, 0), (1, rows)):
-                        if e == edge:
-                            at = v * cols + cols - 1
-                            sx[side, at : at + 1] = ext[v, e, cols - 1 : cols]
-                            at = count * cols + v
-                            sx[side, at : at + 1] = ext[v, e, cols : cols + 1]
-
-    def absorb_edges(count, ext, rx, sent):
+                        add(ext, v, e, row, rc, 2 + side)
+                for side, edge in ((0, 0), (1, rows)):
+                    if out is not None and e == edge:
+                        at = v * cols + cols - 1
+                        out[0][side, at : at + 1] = ext[v, e, cols - 1 : cols]
+                        put(out[1], side, v, ext[v, e, cols : cols + 1])
+
+    def absorb_edges(count, ext, rx, rr, sent):
         for copy in sent:
             copy.wait_recv()
         for v in range(count):
             for side, e in ((0, rows), (1, 0)):
                 ext[v, e, 0:cols] += rx[side, v * cols : (v + 1) * cols]
-                ext[v, e, cols : cols + 1] += rx[side, count * cols + v : count * cols + v + 1]
+                add(ext, v, e, cols, rr, side)
 
     def static_solve(ext):
         for e in range(rows + 1):
@@ -374,14 +388,20 @@
 
     tips = [(sc_s.at[s], rc_s.at[s]) if s + 1 < STEPS else (None, None) for s in range(STEPS)]
     static_sent = [
-        copies(sx_s.at[s], sy_s.at[s], tips[s][0], rx_s.at[s], ry_s.at[s], tips[s][1], 0, s)
+        copies(
+            sx_s.at[s], sy_s.at[s], tips[s][0], sr_s.at[s],
+            rx_s.at[s], ry_s.at[s], tips[s][1], rr_s.at[s], 0, s,
+        )
         for s in range(STEPS)
     ]
     dynamic_sent = [
-        copies(sx_d.at[s], sy_d.at[s], sc_d.at[s], rx_d.at[s], ry_d.at[s], rc_d.at[s], 1, s)
+        copies(
+            sx_d.at[s], sy_d.at[s], sc_d.at[s], sr_d.at[s],
+            rx_d.at[s], ry_d.at[s], rc_d.at[s], rr_d.at[s], 1, s,
+        )
         for s in range(STEPS)
     ]
-    groups = {0: (0, 4, 5), rows: (1, 6, 7)}
+    groups = {0: (0, 4, 6, 7), rows: (1, 5, 8, 9)}
 
     def send_edge(sent, e):
         for k in groups[e]:
@@ -395,13 +415,13 @@
     def build_static(s, edges):
         build(
             load_static(s), translate_static, NS, est.at[s],
-            sx_s.at[s], sy_s.at[s], tips[s][0], edges,
+            sx_s.at[s], sy_s.at[s], tips[s][0], sr_s.at[s], edges,
         )
 
     def build_dynamic(s, edges):
         build(
             load_dynamic(s), translate_dynamic, ND, edy,
-            sx_d.at[s], sy_d.at[s], sc_d.at[s], edges,
+            sx_d.at[s], sy_d.at[s], sc_d.at[s], sr_d.at[s], edges,
         )
 
     inner, every = range(1, rows), range(rows + 1)
@@ -412,16 +432,17 @@
 
     def send_static(s):
         if tips[s][1] is None:
-            absorb_sides(NS, est.at[s], ry_s.at[s], None, sx_s.at[s], static_sent[s][2:], every)
+            out = (sx_s.at[s], sr_s.at[s])
+            absorb_sides(NS, est.at[s], ry_s.at[s], None, out, static_sent[s][2:4], every)
         for e in (0, rows):
             send_edge(static_sent[s], e)
 
     def finish_static(s):
-        absorb_edges(NS, est.at[s], rx_s.at[s], static_sent[s][:2])
+        sent = static_sent[s]
+        absorb_edges(NS, est.at[s], rx_s.at[s], rr_s.at[s], sent[:2] + sent[4:6])
         if tips[s][1] is not None:
-            absorb_sides(
-                NS, est.at[s], ry_s.at[s], tips[s][1], None, static_sent[s][2:], every
-            )
+            late = sent[2:4] + sent[6:]
+            absorb_sides(NS, est.at[s], ry_s.at[s], tips[s][1], None, late, every)
         static_solve(est.at[s])
 
     def absorb_inner(s):
@@ -430,8 +451,8 @@
 
     def absorb_outer(s):
         sent = dynamic_sent[s]
-        absorb_edges(ND, edy, rx_d.at[s], sent[:2])
-        absorb_sides(ND, edy, ry_d.at[s], rc_d.at[s], None, sent[4:], (0, rows))
+        absorb_edges(ND, edy, rx_d.at[s], rr_d.at[s], sent[:2] + sent[4:6])
+        absorb_sides(ND, edy, ry_d.at[s], rc_d.at[s], None, sent[6:], (0, rows))
 
     def at_edge(edge, act):
         for e in (0, rows):
@@ -446,11 +467,12 @@
         send_edge(dynamic_sent[s], e)
 
     shift_load.wait()
-    wait_loads(loads[0][:3])
-    static_sums(lead_row, lead_half, True)
+    for j in range(yb):
+        wait_loads(loads[0][3 * j : 3 * j + 3])
+        static_sums(lead_row, lead_half, True, j * zb, j * zb + zb)
     pl.semaphore_wait(barrier, len(DIRS))
     at_edge(lead_edge, functools.partial(static_edge, 0))
-    wait_loads(loads[0][3:])
+    wait_loads(loads[0][3 * yb :])
     flow_sums(0, lead_row, codes_of(lead_half))
     at_edge(lead_edge, functools.partial(dynamic_edge, 0))
     for group in loads[1:]:
@@ -514,10 +536,12 @@
     plane = (slots, rows, cols, depth)
 
     def faces(count, tip_steps):
-        wide = pltpu.VMEM((STEPS, 2, count * cols + pad8(count), depth), F32)
+        lines = pad8(count * (depth // 128))
+        wide = pltpu.VMEM((STEPS, 2, pad8(count * cols), depth), F32)
         thin = pltpu.VMEM((STEPS, 2, pad8((rows + 1) * count), depth), F32)
-        tips = pltpu.VMEM((tip_steps, 4, pad8(count), depth), F32)
-        return [wide, thin, tips] * 2
+        tips = pltpu.VMEM((tip_steps, 4, lines, 128), F32)
+        rims = pltpu.VMEM((STEPS, 2, lines, 128), F32)
+        return [wide, thin, tips, rims] * 2
 
     hbm = pl.BlockSpec(memory_space=pltpu.HBM)
     return pl.pallas_call(
@@ -541,9 +565,9 @@
             *faces(NS, STEPS - 1),
             *faces(ND, STEPS),
             pltpu.SemaphoreType.DMA((1,)),
-            pltpu.SemaphoreType.DMA((rows, 5)),
-            pltpu.SemaphoreType.DMA((2, STEPS, len(DIRS))),
-            pltpu.SemaphoreType.DMA((2, STEPS, len(DIRS))),
+            pltpu.SemaphoreType.DMA((rows, 3 * (cols // 8) + 2)),
+            pltpu.SemaphoreType.DMA((2, STEPS, len(DIRS) + 2)),
+            pltpu.SemaphoreType.DMA((2, STEPS, len(DIRS) + 2)),
         ],
         compiler_params=pltpu.CompilerParams(
             collective_id=0, has_side_effects=True, vmem_limit_bytes=40000000

time: 31.2 us -> 30.8 us (0.987)
  Pallas kernels: 30 us -> 29.5 us
    pallas_call x1, Pallas kernels: 30 us -> 29.5 us  [local(): pl.pallas_call(kernel, out_shape=pltpu.VMEM(full, F32), in_specs=[hbm] *...]
where the time goes in v4:
time: 30.8 us; the launch traced here: 30.5 us
  Pallas kernels  29.5 us (96%)
  local copies, waits for them, and re-layouts  1.02 us (3%)
    pallas_call x1, Pallas kernels, local(): pl.pallas_call(kernel, out_shape=pltpu.VMEM(full, F32), in_specs=[hbm] *...  29.5 us
    unnamed x1, local copies, waits for them, and re-layouts  1.02 us

profile of v4, /device:TPU:1, one launch (start us, length us, event | category | flops | bytes accessed | tf_op | source)
XLA Modules:
  0.0 30.5 jit_solution(11841134048320928843)
XLA Ops:
  0.0 29.5 %shard_map.64 = f32[3,12,2,16,256]{4,3,2,1,0:T(8,128)S(1)} custom-call(s32[3]{0:T(128)} %shift_h.1, f32[3,12,2,16,256]{4,3,2,1,0:T(8,128)} %pos_h.1, f32[3,12,2,16,256]{4,3,2,1,0:T(8,128)} %vel_h.1, f32[3,12,2,16,256]{4,3,2,1,0:T(8,128)} %th_h.1, s32[12,2,16,256]{3,2,1,0:T(8,128)} %off_h.1, s32[12,2,16,256]{3,2,1,0:T(8,128)} %occ_h.1), custom_call_target="tpu_custom_call" | custom-call | tf_op jit(solution)/shard_map/pallas_call | solution.py:547
  29.5 1.0 %copy.8 = f32[3,12,2,16,256]{4,3,2,1,0:T(8,128)} copy(f32[3,12,2,16,256]{4,3,2,1,0:T(8,128)S(1)} %shard_map.64) | data formatting | bytes 2359296
